TPU v7x, 32 devices: a whole 2x2x4 slice. The times are simulated.
32 devices in a mesh: fsdp: 8 (over z, y), rep: 4 (over x, core).
Axes of the slice: x: 2, y: 2, z: 4, core: 2. Of those that a mesh axis runs over, the one named last changes fastest.
Arguments:
- latents: float32 [192, 4, 1024], P(('fsdp', 'rep')), may hold values from -6 to 6
- tsteps: int32 [192], P(('fsdp', 'rep')), may hold values from 0 to 999
- labels: int32 [192], P(('fsdp', 'rep')), may hold values from 0 to 1000
- noise: float32 [192, 4, 1024], P(('fsdp', 'rep')), may hold values from -6 to 6
- layer_in: float32 [2, 384, 5376], P(None, 'fsdp'), may hold values from -0.3125 to 0.3125
- layer_out: float32 [2, 1536, 384], P(None, 'fsdp'), may hold values from -0.15625 to 0.15625
- edge_mat: float32 [384, 2457], P('fsdp'), may hold values from -4 to 4
- layer_bias: float32 [2, 5376], replicated, may hold values from -2 to 2
- top_bias: float32 [1952], replicated, may hold values from -2 to 2
- in_rows: float32 [2, 384], P(None, 'fsdp'), may hold values from 0.0005 to 0.2
- in_cols: float32 [2, 5376], replicated, may hold values from 0.005 to 0.05
- out_rows: float32 [2, 1536], P(None, 'fsdp'), may hold values from 0.0005 to 0.2
- out_cols: float32 [2, 384], replicated, may hold values from 0.005 to 0.05
- edge_rows: float32 [384], P('fsdp'), may hold values from 0.0005 to 0.2
- edge_cols: float32 [2457], replicated, may hold values from 0.005 to 0.05
- layer_bias_v: float32 [2, 5376], replicated, may hold values from 0.005 to 0.05
- top_bias_v: float32 [1952], replicated, may hold values from 0.005 to 0.05
Outputs:
- loss: float32 [], replicated
- layer_in_new: float32 [2, 384, 5376], P(None, 'fsdp')
- layer_out_new: float32 [2, 1536, 384], P(None, 'fsdp')
- edge_mat_new: float32 [384, 2457], P('fsdp')
- layer_bias_new: float32 [2, 5376], replicated
- top_bias_new: float32 [1952], replicated
- in_rows_new: float32 [2, 384], P(None, 'fsdp')
- in_cols_new: float32 [2, 5376], replicated
- out_rows_new: float32 [2, 1536], P(None, 'fsdp')
- out_cols_new: float32 [2, 384], replicated
- edge_rows_new: float32 [384], P('fsdp')
- edge_cols_new: float32 [2457], replicated
- layer_bias_v_new: float32 [2, 5376], replicated
- top_bias_v_new: float32 [1952], replicated
- clip_roots: float32 [5], replicated
All inputs are finite; a program needn't handle non-finite values.
Results may differ from a plain program's by a relative error of at most 0.0015.
The roundings to bfloat16 on the way count: a program that leaves them out, or rounds other values in their place, can miss the bound.
Values may be sent and summed in bfloat16 or wider, within the bound.
A program may use at most 256 MiB of HBM per device.

v0:
```python
import math
import jax
import jax.numpy as jnp
from jax import lax
from jax.sharding import PartitionSpec as P

D = 384
HEADS = 6
HEAD_DIM = 64
FF = 1536
CHANNELS = 4
PATCH = 2
GRID = 32
TSTEPS = 1000
NCLS = 1001
FREQ = 256
MICRO = 3
PATCH_IN = 16
eps_norm = 1e-06
eps_stat = 1e-30
decay = 0.5
rate = 0.01
clip_level = 1.0


def round_value(values):
    return lax.optimization_barrier(values.astype(jnp.bfloat16)).astype(jnp.float32)


def rounders():
    rounding = jax.custom_vjp(round_value)

    def keep_forward(values):
        return (round_value(values), None)

    def pass_backward(kept, grad):
        return (grad,)

    rounding.defvjp(keep_forward, pass_backward)

    def unchanged(values):
        return values

    backing = jax.custom_vjp(unchanged)

    def back_forward(values):
        return (values, None)

    def back_backward(kept, grad):
        return (round_value(grad),)

    backing.defvjp(back_forward, back_backward)
    return (rounding, backing)


def low(values):
    return rounders()[0](values)


def low_back(values):
    return rounders()[1](values)


def mult(left, right, form):
    return jnp.einsum(form, left, right, preferred_element_type=jnp.float32)


def normalize(values):
    center = values - jnp.mean(values, axis=-1, keepdims=True)
    spread = jnp.mean(center * center, axis=-1, keepdims=True)
    return center * lax.rsqrt(spread + eps_norm)


def mix_weights(tsteps):
    betas = 0.0001 + (0.02 - 0.0001) * jnp.arange(TSTEPS, dtype=jnp.float32) / (TSTEPS - 1)
    alpha_bar = jnp.exp(jnp.cumsum(jnp.log(1.0 - betas)))
    picked = jnp.arange(TSTEPS)[None, :] == tsteps[:, None]
    return jnp.sum(jnp.where(picked, alpha_bar[None, :], 0.0), axis=1)


def patchify(latent_rows):
    images = latent_rows.shape[0]
    grid_side = GRID // PATCH
    shaped = latent_rows.reshape(images, CHANNELS, grid_side, PATCH, grid_side, PATCH)
    shaped = jnp.transpose(shaped, (0, 2, 4, 1, 3, 5))
    return shaped.reshape(images, grid_side * grid_side, CHANNELS * PATCH * PATCH)


def position_table():
    grid_side = GRID // PATCH
    quarter = D // 4
    omegas = 1.0 / 10000.0 ** (jnp.arange(quarter, dtype=jnp.float32) / quarter)
    places = jnp.arange(grid_side * grid_side)
    across = (places % grid_side).astype(jnp.float32)
    downward = (places // grid_side).astype(jnp.float32)

    def one_axis(coords):
        angles = coords[:, None] * omegas[None, :]
        return jnp.concatenate([jnp.sin(angles), jnp.cos(angles)], axis=1)

    return jnp.concatenate([one_axis(across), one_axis(downward)], axis=1)


def time_features(tsteps):
    half_freq = FREQ // 2
    frequencies = jnp.exp(-math.log(10000.0) * jnp.arange(half_freq, dtype=jnp.float32) / half_freq)
    angles = tsteps.astype(jnp.float32)[:, None] * frequencies[None, :]
    return jnp.concatenate([jnp.cos(angles), jnp.sin(angles)], axis=1)


def block(tokens, condition, weights, weights_down, biases):
    images = tokens.shape[0]
    tok_count = tokens.shape[1]
    modulation = low_back(mult(condition, weights[:, : 6 * D], "bd,de->be") + biases[: 6 * D])
    shift_attn = modulation[:, 0:D][:, None]
    scale_attn = modulation[:, D : 2 * D][:, None]
    gate_attn = modulation[:, 2 * D : 3 * D][:, None]
    shift_mlp = modulation[:, 3 * D : 4 * D][:, None]
    scale_mlp = modulation[:, 4 * D : 5 * D][:, None]
    gate_mlp = modulation[:, 5 * D : 6 * D][:, None]
    normed = low(normalize(tokens) * (1.0 + scale_attn) + shift_attn)
    bias_qkv = jnp.concatenate(
        [biases[6 * D : 7 * D], jnp.zeros_like(biases[:D]), biases[7 * D : 8 * D]]
    )
    project = low(low_back(mult(normed, weights[:, 6 * D : 9 * D], "btd,de->bte") + bias_qkv))
    queries = project[..., :D].reshape(images, tok_count, HEADS, HEAD_DIM)
    keys_all = project[..., D : 2 * D].reshape(images, tok_count, HEADS, HEAD_DIM)
    values_all = project[..., 2 * D :].reshape(images, tok_count, HEADS, HEAD_DIM)
    scores = low_back(mult(queries, keys_all, "bqhe,bkhe->bhqk") * HEAD_DIM ** (-0.5))
    weights_soft = low(jax.nn.softmax(scores, axis=-1))
    attended = low(low_back(mult(weights_soft, values_all, "bhqk,bkhe->bqhe"))).reshape(
        images, tok_count, D
    )
    branch = low_back(
        mult(attended, weights[:, 9 * D : 10 * D], "btd,de->bte") + biases[8 * D : 9 * D]
    )
    tokens = tokens + gate_attn * branch
    normed_mlp = low(normalize(tokens) * (1.0 + scale_mlp) + shift_mlp)
    inner = low_back(
        mult(normed_mlp, weights[:, 10 * D :], "btd,df->btf") + biases[9 * D : 9 * D + FF]
    )
    activated = low(jax.nn.gelu(inner, approximate=True))
    outward = low_back(mult(activated, weights_down, "btf,fd->btd") + biases[9 * D + FF :])
    return tokens + gate_mlp * outward


def image_loss(params, latents, tsteps, labels, noise):
    layer_in, layer_out, edge_mat, layer_bias, top_bias = params
    depth = layer_in.shape[0]
    alphas = mix_weights(tsteps)
    noisy = (
        jnp.sqrt(alphas)[:, None, None] * latents + jnp.sqrt(1.0 - alphas)[:, None, None] * noise
    )
    patches = low(patchify(noisy))
    target = patchify(noise)
    edge_low = low(edge_mat)
    start_freq = NCLS + PATCH_IN
    start_tail = start_freq + FREQ
    class_cols = edge_low[:, :NCLS]
    patch_cols = edge_low[:, NCLS:start_freq]
    freq_cols = edge_low[:, start_freq:start_tail]
    time_second = edge_low[:, start_tail : start_tail + D]
    final_cols = edge_low[:, start_tail + D : start_tail + 3 * D]
    head_cols = edge_low[:, start_tail + 3 * D :]
    tokens = (
        low_back(mult(patches, patch_cols, "btp,dp->btd") + top_bias[:D]) + position_table()[None]
    )
    features = low(time_features(tsteps))
    time_first = low_back(mult(features, freq_cols, "bf,df->bd") + top_bias[D : 2 * D])
    time_out = low_back(
        mult(low(jax.nn.silu(time_first)), time_second, "bd,de->be") + top_bias[2 * D : 3 * D]
    )
    class_emb = jnp.take(class_cols, labels, axis=1).T
    condition = low(jax.nn.silu(time_out + class_emb))
    for layer_index in range(depth):
        tokens = block(
            tokens,
            condition,
            low(layer_in[layer_index]),
            low(layer_out[layer_index]),
            layer_bias[layer_index],
        )
    closing = low_back(mult(condition, final_cols, "bd,de->be") + top_bias[3 * D : 5 * D])
    normed = low(normalize(tokens) * (1.0 + closing[:, None, D:]) + closing[:, None, :D])
    predicted = low_back(mult(normed, head_cols, "btd,dp->btp") + top_bias[5 * D :])
    misfit = predicted[..., :PATCH_IN] - target
    return jnp.sum(misfit * misfit)


def fetch_weights(layer_in, layer_out, edge_mat, again):
    gathered_in = []
    gathered_out = []
    for layer_index in range(layer_in.shape[0]):
        own_in = layer_in[layer_index].astype(jnp.bfloat16)
        own_out = layer_out[layer_index].astype(jnp.bfloat16)
        if again:
            full_in, full_out = (
                lax.all_gather(own_in, "fsdp", axis=0, tiled=True),
                lax.all_gather(own_out, "fsdp", axis=0, tiled=True),
            )
        else:
            full_in, full_out = (
                lax.all_gather(own_in, "fsdp", axis=0, tiled=True),
                lax.all_gather(own_out, "fsdp", axis=0, tiled=True),
            )
        gathered_in.append(full_in)
        gathered_out.append(full_out)
    if again:
        full_edge = lax.all_gather(edge_mat.astype(jnp.bfloat16), "fsdp", axis=0, tiled=True)
    else:
        full_edge = lax.all_gather(edge_mat.astype(jnp.bfloat16), "fsdp", axis=0, tiled=True)
    return (
        jnp.stack(gathered_in).astype(jnp.float32),
        jnp.stack(gathered_out).astype(jnp.float32),
        full_edge.astype(jnp.float32),
    )


def step_of(grad, rows_new, cols_new, rows_mean):
    second = rows_new[:, :, None] * cols_new[:, None, :] / rows_mean[:, None, None]
    return grad * lax.rsqrt(second)


def plain(weight, grad, moment):
    moment_new = decay * moment + (1.0 - decay) * (grad * grad + eps_stat)
    update = grad * lax.rsqrt(moment_new)
    root = jnp.sqrt(jnp.mean(update * update, axis=-1, keepdims=True))
    return (weight - rate * update / jnp.maximum(1.0, root / clip_level), moment_new)


def shards(
    latents,
    tsteps,
    labels,
    noise,
    layer_in,
    layer_out,
    edge_mat,
    layer_bias,
    top_bias,
    in_rows,
    in_cols,
    out_rows,
    out_cols,
    edge_rows,
    edge_cols,
    layer_bias_v,
    top_bias_v,
):
    per_micro = latents.shape[0] // MICRO
    loss_sum = jnp.zeros((), jnp.float32)
    gradients = None

    def add_grads(total_grads, grads_now):
        if total_grads is None:
            return grads_now
        return jax.tree.map(jnp.add, total_grads, grads_now)

    for micro_index in range(MICRO):
        start = micro_index * per_micro
        data_now = (
            latents[start : start + per_micro],
            tsteps[start : start + per_micro],
            labels[start : start + per_micro],
            noise[start : start + per_micro],
        )
        full_in, full_out, full_edge = fetch_weights(layer_in, layer_out, edge_mat, False)
        loss_part = image_loss((full_in, full_out, full_edge, layer_bias, top_bias), *data_now)
        loss_sum = loss_sum + loss_part
        again_in, again_out, again_edge = fetch_weights(layer_in, layer_out, edge_mat, True)
        params = (again_in, again_out, again_edge, layer_bias, top_bias)
        recomputed, pullback = jax.vjp(lambda params_now: image_loss(params_now, *data_now), params)
        (grads_now,) = pullback(jnp.ones_like(recomputed))
        gradients = add_grads(gradients, grads_now)
    grad_in_full, grad_out_full, grad_edge_full, grad_lbias, grad_tbias = gradients
    shard_in, shard_out, shard_edge = (
        lax.psum_scatter(grad_in_full, "fsdp", scatter_dimension=1, tiled=True),
        lax.psum_scatter(grad_out_full, "fsdp", scatter_dimension=1, tiled=True),
        lax.psum_scatter(grad_edge_full[None], "fsdp", scatter_dimension=1, tiled=True),
    )
    shard_in, shard_out, shard_edge = lax.psum((shard_in, shard_out, shard_edge), "rep")
    bias_in_sum, bias_top_sum, loss_total = lax.psum(
        (grad_lbias, grad_tbias, loss_sum), ("fsdp", "rep")
    )
    fsdp_count = lax.axis_size("fsdp")
    tok_total = latents.shape[0] * fsdp_count * lax.axis_size("rep") * (GRID // PATCH) ** 2
    scale_grad = 1.0 / (PATCH_IN * math.sqrt(tok_total))
    loss = loss_total / (tok_total * PATCH_IN)
    grad_in = shard_in * scale_grad
    grad_out = shard_out * scale_grad
    grad_edge = shard_edge * scale_grad
    full_rows_in = layer_in.shape[1] * fsdp_count
    full_rows_out = layer_out.shape[1] * fsdp_count
    full_rows_edge = edge_mat.shape[0] * fsdp_count
    square_in = grad_in * grad_in + eps_stat
    square_out = grad_out * grad_out + eps_stat
    square_edge = grad_edge * grad_edge + eps_stat
    rows_in_new = decay * in_rows + (1.0 - decay) * jnp.mean(square_in, axis=2)
    rows_out_new = decay * out_rows + (1.0 - decay) * jnp.mean(square_out, axis=2)
    rows_edge_new = decay * edge_rows[None] + (1.0 - decay) * jnp.mean(square_edge, axis=2)
    col_in, total_in, col_out, total_out, col_edge, total_edge = lax.psum(
        (
            jnp.sum(square_in, axis=1),
            jnp.sum(rows_in_new, axis=1),
            jnp.sum(square_out, axis=1),
            jnp.sum(rows_out_new, axis=1),
            jnp.sum(square_edge, axis=1),
            jnp.sum(rows_edge_new, axis=1),
        ),
        "fsdp",
    )
    cols_in_new = decay * in_cols + (1.0 - decay) * col_in / full_rows_in
    cols_out_new = decay * out_cols + (1.0 - decay) * col_out / full_rows_out
    cols_edge_new = decay * edge_cols[None] + (1.0 - decay) * col_edge / full_rows_edge
    update_in = step_of(grad_in, rows_in_new, cols_in_new, total_in / full_rows_in)
    update_out = step_of(grad_out, rows_out_new, cols_out_new, total_out / full_rows_out)
    update_edge = step_of(grad_edge, rows_edge_new, cols_edge_new, total_edge / full_rows_edge)
    sum_in, sum_out, sum_edge = lax.psum(
        (
            jnp.sum(update_in * update_in, axis=(1, 2)),
            jnp.sum(update_out * update_out, axis=(1, 2)),
            jnp.sum(update_edge * update_edge, axis=(1, 2)),
        ),
        "fsdp",
    )
    mean_sq_in = sum_in / (full_rows_in * grad_in.shape[2])
    mean_sq_out = sum_out / (full_rows_out * grad_out.shape[2])
    mean_sq_edge = sum_edge / (full_rows_edge * grad_edge.shape[2])
    roots_in = jnp.sqrt(mean_sq_in)
    roots_out = jnp.sqrt(mean_sq_out)
    roots_edge = jnp.sqrt(mean_sq_edge)
    factor_in = jnp.maximum(1.0, roots_in / clip_level)[:, None, None]
    factor_out = jnp.maximum(1.0, roots_out / clip_level)[:, None, None]
    factor_edge = jnp.maximum(1.0, roots_edge / clip_level)[:, None, None]
    in_new = layer_in - rate * update_in / factor_in
    out_new = layer_out - rate * update_out / factor_out
    edge_new = (edge_mat[None] - rate * update_edge / factor_edge)[0]
    clip_roots = jnp.concatenate([roots_in, roots_out, roots_edge])
    lbias_new, lbias_v_new = plain(layer_bias, bias_in_sum * scale_grad, layer_bias_v)
    tbias_new, tbias_v_new = plain(top_bias, bias_top_sum * scale_grad, top_bias_v)
    return (
        loss,
        in_new,
        out_new,
        edge_new,
        lbias_new,
        tbias_new,
        rows_in_new,
        cols_in_new,
        rows_out_new,
        cols_out_new,
        rows_edge_new[0],
        cols_edge_new[0],
        lbias_v_new,
        tbias_v_new,
        clip_roots,
    )


def solution(mesh):
    placed = (
        P(("fsdp", "rep"), None, None),
        P(("fsdp", "rep")),
        P(("fsdp", "rep")),
        P(("fsdp", "rep"), None, None),
        P(None, "fsdp", None),
        P(None, "fsdp", None),
        P("fsdp", None),
        P(),
        P(),
        P(None, "fsdp"),
        P(),
        P(None, "fsdp"),
        P(),
        P("fsdp"),
        P(),
        P(),
        P(),
    )
    return jax.shard_map(
        shards,
        mesh=mesh,
        in_specs=placed,
        out_specs=(
            P(),
            P(None, "fsdp", None),
            P(None, "fsdp", None),
            P("fsdp", None),
            P(),
            P(),
            P(None, "fsdp"),
            P(),
            P(None, "fsdp"),
            P(),
            P("fsdp"),
            P(),
            P(),
            P(),
            P(),
        ),
        check_vma=False,
    )
```

profile of v0, /device:TPU:0, one launch (start us, length us, event | category | flops | bytes accessed | tf_op | source)
XLA Modules:
  0.0 1379.7 jit_solution(4260965202607381053)
XLA Ops:
  37.3 16.8 %all-gather.18.cloned.1.call-done = bf16[1,1536,384]{2,1,0:T(8,128)(2,1)} async-done(((bf16[1,192,384]{2,1,0:T(8,128)(2,1)}), bf16[1,1536,384]{2,1,0:T(8,128)(2,1)}) %all-gather.18.cloned.1.call-update) | async-done | bytes 1179664 | tf_op jit(solution)/shard_map/all_gather | solution.py:204
  54.1 42.0 %all-gather.14.cloned.1.call-done = bf16[1,1536,384]{2,1,0:T(8,128)(2,1)} async-done(((bf16[1,192,384]{2,1,0:T(8,128)(2,1)}), bf16[1,1536,384]{2,1,0:T(8,128)(2,1)}) %all-gather.14.cloned.1.call-update) | async-done | bytes 1179664 | tf_op jit(solution)/shard_map/all_gather | solution.py:204
  96.1 48.7 %all-gather.10.cloned.1.call-done = bf16[384,2457]{1,0:T(8,128)(2,1)} async-done(((bf16[48,2457]{1,0:T(8,128)(2,1)}), bf16[384,2457]{1,0:T(8,128)(2,1)}) %all-gather.10.cloned.1.call-update) | async-done | bytes 1886992 | tf_op jit(solution)/shard_map/all_gather | solution.py:211
  166.5 51.5 %all-gather.12.cloned.1.call-done = bf16[1,384,5376]{2,1,0:T(8,128)(2,1)} async-done(((bf16[1,48,5376]{2,1,0:T(8,128)(2,1)}), bf16[1,384,5376]{2,1,0:T(8,128)(2,1)}) %all-gather.12.cloned.1.call-update) | async-done | bytes 4128784 | tf_op jit(solution)/shard_map/all_gather | solution.py:203
  223.5 67.7 %all-gather.16.cloned.1.call-done = bf16[1,384,5376]{2,1,0:T(8,128)(2,1)} async-done(((bf16[1,48,5376]{2,1,0:T(8,128)(2,1)}), bf16[1,384,5376]{2,1,0:T(8,128)(2,1)}) %all-gather.16.cloned.1.call-update) | async-done | bytes 4128784 | tf_op jit(solution)/shard_map/all_gather | solution.py:203
  315.2 2.6 fusion.391
  340.5 4.7 multiply_convert_fusion.9
  355.5 4.9 fusion.389
  367.2 3.2 multiply_convert_fusion.8
  376.0 4.6 multiply_convert_fusion.7
  389.3 4.7 fusion.386
  402.6 5.0 multiply_convert_fusion.11
  417.7 4.7 fusion.392
  429.2 3.2 multiply_convert_fusion.10
  435.2 3.2 multiply_convert_fusion.6
  467.6 3.1 fusion.162
  470.7 2.9 multiply_reduce_fusion.3
  479.0 2.8 fusion.47
  481.9 2.9 multiply_reduce_fusion.29
  492.6 3.0 fusion.154
  495.7 2.9 multiply_reduce_fusion.1
  521.7 3.7 multiply_reduce_fusion.35
  537.4 2.9 fusion.40
  540.5 3.0 multiply_reduce_fusion.23
  551.9 3.0 fusion.150
  554.9 2.9 multiply_reduce_fusion
  568.8 3.0 fusion.158
  578.8 2.7 fusion.19
  581.7 2.9 multiply_reduce_fusion.53
  592.4 3.0 fusion.170
  607.2 2.8 fusion.12
  610.1 2.9 multiply_reduce_fusion.47
  620.8 3.0 fusion.166
  687.2 6.5 add_bitcast_fusion.6
  693.7 9.1 copy.871
  726.4 2.7 add_add_fusion.1
  761.3 3.3 add_bitcast_fusion.2
  764.7 5.1 add_bitcast_fusion
  769.8 12.6 add_bitcast_fusion.4
  782.4 11.1 add_bitcast_fusion.1
  793.5 20.9 %add_add_fusion = f32[2,384,5376]{2,1,0:T(8,128)} fusion(f32[1,384,5376]{2,1,0:T(8,128)} %add_bitcast_fusion, f32[1,384,5376]{2,1,0:T(8,128)} %get-tuple-element.452, f32[1,384,5376]{2,1,0:T(8,128)S(1)} %add_bitcast_fusion.2, f32[1,384,5376]{2,1,0:T(8,128)} %get-tuple-element.453, f32[1,384,5376]{2,1,0:T(8,128)} %get-tuple-element.454, ...), kind=kLoop, calls=%fused_computation.15 | loop fusion | flops 20643840 | bytes 66060288 | tf_op jit(solution)/shard_map/add | solution.py:257
  830.7 40.9 %all-reduce.176 = (f32[]{:T(128)}, f32[2,5376]{1,0:T(2,128)S(1)}, f32[1952]{0:T(1024)S(1)}) all-reduce(f32[]{:T(128)S(6)} %add.2146, f32[2,5376]{1,0:T(2,128)S(1)} %add_add_fusion.26, f32[1952]{0:T(1024)S(1)} %add_add_fusion.27), channel_id=1, replica_groups=mesh['fsdp'=8,'rep'=4] {'fsdp','rep'}, use_global_device_ids=true, to_apply=%region_50.52 | all-reduce | flops 12705 | bytes 101640 | tf_op jit(solution)/shard_map/psum | solution.py:282
  876.3 73.4 %reduce-scatter.5.cloned.1.call-done = f32[2,192,384]{2,1,0:T(8,128)} async-done(((f32[2,1536,384]{2,1,0:T(8,128)}), f32[2,192,384]{2,1,0:T(8,128)}) %reduce-scatter.5.cloned.1.call-update) | async-done | bytes 589840 | tf_op jit(solution)/shard_map/reduce_scatter | solution.py:278
  949.7 279.4 %reduce-scatter.3.cloned.1.call-done = f32[2,48,5376]{2,1,0:T(8,128)} async-done(((f32[2,384,5376]{2,1,0:T(8,128)}), f32[2,48,5376]{2,1,0:T(8,128)}) %reduce-scatter.3.cloned.1.call-update) | async-done | bytes 2064400 | tf_op jit(solution)/shard_map/reduce_scatter | solution.py:277
  1229.9 69.9 %all-reduce.185.cloned.1.call-done = (f32[2,48,5376]{2,1,0:T(8,128)}, f32[2,192,384]{2,1,0:T(8,128)}, f32[1,48,2457]{2,1,0:T(8,128)}) async-done(((f32[2,48,5376]{2,1,0:T(8,128)}, f32[2,192,384]{2,1,0:T(8,128)}, f32[1,48,2457]{2,1,0:T(8,128)}), (f32[2,48,5376]{2,1,0:T(8,128)}, f32[2,192,384]{2,1,0:T(8,128)}, f32[1,48,2457]{2,1,0:T(8,128)})) %all-reduce.185.cloned.1.call-update) | async-done | bytes 3125968 | tf_op jit(solution)/shard_map/psum | solution.py:281
  1305.7 37.6 %all-reduce.178 = (f32[2]{0:T(128)S(1)}, f32[2,5376]{1,0:T(2,128)S(1)}, f32[2]{0:T(128)S(1)}, f32[2,384]{1,0:T(2,128)S(1)}, f32[1]{0:T(128)}, /*index=5*/f32[1,2457]{1,0:T(1,128)S(1)}) all-reduce(f32[2]{0:T(128)S(1)} %get-tuple-element.165, f32[2,5376]{1,0:T(2,128)S(1)} %get-tuple-element.73, ...), channel_id=1, replica_groups=mesh['fsdp'=8,'rep'=4] {'fsdp'}, use_global_device_ids=true, to_apply=%region_159.162 | all-reduce | flops 13982 | bytes 111856 | tf_op jit(solution)/shard_map/psum | solution.py:301
  1346.0 17.8 %all-reduce.177 = (f32[2]{0:T(128)S(1)}, f32[2]{0:T(128)S(1)}, f32[1]{0:T(128)}) all-reduce(f32[2]{0:T(128)S(1)} %multiply_reduce_fusion.12, f32[2]{0:T(128)S(1)} %multiply_reduce_fusion.70, f32[1]{0:T(128)} %bitcast.206), channel_id=1, replica_groups=mesh['fsdp'=8,'rep'=4] {'fsdp'}, use_global_device_ids=true, to_apply=%region_161.164 | all-reduce | flops 5 | bytes 40 | tf_op jit(solution)/shard_map/psum | solution.py:318
  1366.5 3.6 divide_subtract_fusion
  (1743 shorter events, 437.1 us)
Async XLA Ops:
  7.2 46.9 %all-gather.18.cloned.1.call-start = ((), (), s32[]{:S(2)}) async-start(), calls=%async_computation.8 | async-start | bytes 1327104 | tf_op jit(solution)/shard_map/all_gather | solution.py:204
  9.3 86.8 %all-gather.14.cloned.1.call-start = ((), (), s32[]{:S(2)}) async-start(), calls=%async_computation.6 | async-start | bytes 1327104 | tf_op jit(solution)/shard_map/all_gather | solution.py:204
  10.0 134.7 %all-gather.10.cloned.1.call-start = ((), (), s32[]{:S(2)}) async-start(), calls=%async_computation.2 | async-start | bytes 2211840 | tf_op jit(solution)/shard_map/all_gather | solution.py:211
  11.9 206.1 %all-gather.12.cloned.1.call-start = ((), (), s32[]{:S(2)}) async-start(), calls=%async_computation.5 | async-start | bytes 4644864 | tf_op jit(solution)/shard_map/all_gather | solution.py:203
  13.1 278.0 %all-gather.16.cloned.1.call-start = ((), (), s32[]{:S(2)}) async-start(), calls=%async_computation.7 | async-start | bytes 4644864 | tf_op jit(solution)/shard_map/all_gather | solution.py:203
  13.7 860.6 %all-reduce.183.cloned.1.call-start = ((), (), s32[]{:S(2)}) async-start(), calls=%async_computation.9 | async-start | bytes 7864320
  17.3 132.3 %copy-start.553 = (bf16[2,256]{1,0:T(2,128)(2,1)}, bf16[2,256]{1,0:T(2,128)(2,1)S(1)}, u32[]{:S(2)}) copy-start(bf16[2,256]{1,0:T(2,128)(2,1)S(1)} %pad_maximum_fusion.3) | copy-start | bytes 3076
  17.3 128.6 %copy-start.555 = (bf16[2,256]{1,0:T(2,128)(2,1)}, bf16[2,256]{1,0:T(2,128)(2,1)S(1)}, u32[]{:S(2)}) copy-start(bf16[2,256]{1,0:T(2,128)(2,1)S(1)} %pad_maximum_fusion.4) | copy-start | bytes 3076
  17.3 130.4 %copy-start.557 = (bf16[2,256]{1,0:T(2,128)(2,1)}, bf16[2,256]{1,0:T(2,128)(2,1)S(1)}, u32[]{:S(2)}) copy-start(bf16[2,256]{1,0:T(2,128)(2,1)S(1)} %pad_maximum_fusion.5) | copy-start | bytes 3076
  160.5 140.3 %copy-start.12 = (f32[2,256,384]{2,1,0:T(8,128)}, f32[2,256,384]{2,1,0:T(8,128)S(1)}, u32[]{:S(2)}) copy-start(f32[2,256,384]{2,1,0:T(8,128)S(1)} %get-tuple-element.368) | copy-start | bytes 2359300
  160.5 140.3 %copy-start.326 = (f32[2,256]{1,0:T(2,128)}, f32[2,256]{1,0:T(2,128)S(1)}, u32[]{:S(2)}) copy-start(f32[2,256]{1,0:T(2,128)S(1)} %broadcast_multiply_fusion.10) | copy-start | bytes 6148
  160.8 57.2 %copy-start.258 = (f32[2304]{0:T(1024)S(1)}, f32[2304]{0:T(1024)}, u32[]{:S(2)}) copy-start(f32[2304]{0:T(1024)} %get-tuple-element.135) | copy-start | bytes 27652
  162.0 138.6 %copy-start.15 = (f32[2,256,384]{2,1,0:T(8,128)}, f32[2,256,384]{2,1,0:T(8,128)S(1)}, u32[]{:S(2)}) copy-start(f32[2,256,384]{2,1,0:T(8,128)S(1)} %get-tuple-element.351) | copy-start | bytes 2359300
  162.0 138.6 %copy-start.328 = (f32[2,256]{1,0:T(2,128)}, f32[2,256]{1,0:T(2,128)S(1)}, u32[]{:S(2)}) copy-start(f32[2,256]{1,0:T(2,128)S(1)} %broadcast_multiply_fusion.5) | copy-start | bytes 6148
  162.8 137.5 %copy-start.9 = (f32[2,256,384]{2,1,0:T(8,128)}, f32[2,256,384]{2,1,0:T(8,128)S(1)}, u32[]{:S(2)}) copy-start(f32[2,256,384]{2,1,0:T(8,128)S(1)} %get-tuple-element.385) | copy-start | bytes 2359300
  162.8 137.5 %copy-start.324 = (f32[2,256]{1,0:T(2,128)}, f32[2,256]{1,0:T(2,128)S(1)}, u32[]{:S(2)}) copy-start(f32[2,256]{1,0:T(2,128)S(1)} %broadcast_multiply_fusion.15) | copy-start | bytes 6148
  163.1 137.8 %copy-start.425 = (f32[2,256]{1,0:T(2,128)}, f32[2,256]{1,0:T(2,128)S(1)}, u32[]{:S(2)}) copy-start(f32[2,256]{1,0:T(2,128)S(1)} %fusion.287) | copy-start | bytes 6148
  163.6 137.0 %copy-start.427 = (f32[2,256]{1,0:T(2,128)}, f32[2,256]{1,0:T(2,128)S(1)}, u32[]{:S(2)}) copy-start(f32[2,256]{1,0:T(2,128)S(1)} %fusion.292) | copy-start | bytes 6148
  163.6 136.7 %copy-start.423 = (f32[2,256]{1,0:T(2,128)}, f32[2,256]{1,0:T(2,128)S(1)}, u32[]{:S(2)}) copy-start(f32[2,256]{1,0:T(2,128)S(1)} %fusion.282) | copy-start | bytes 6148
  164.0 57.7 %copy-start.293 = (bf16[2,384]{1,0:T(2,128)(2,1)S(1)}, bf16[2,384]{1,0:T(2,128)(2,1)}, u32[]{:S(2)}) copy-start(bf16[2,384]{1,0:T(2,128)(2,1)} %copy-done.292) | copy-start | bytes 4612
  165.9 125.2 %copy-start.297 = (bf16[2,384]{1,0:T(2,128)(2,1)S(1)}, bf16[2,384]{1,0:T(2,128)(2,1)}, u32[]{:S(2)}) copy-start(bf16[2,384]{1,0:T(2,128)(2,1)} %copy-done.296) | copy-start | bytes 4612
  219.8 73.2 %copy-start.301 = (bf16[2,384]{1,0:T(2,128)(2,1)S(1)}, bf16[2,384]{1,0:T(2,128)(2,1)}, u32[]{:S(2)}) copy-start(bf16[2,384]{1,0:T(2,128)(2,1)} %copy-done.300) | copy-start | bytes 4612
  434.4 13.0 copy-start.44
  434.4 13.0 copy-start.310
  702.9 246.8 %reduce-scatter.5.cloned.1.call-start = ((), (), s32[]{:S(2)}) async-start(), calls=%async_computation.4 | async-start | bytes 5308416 | tf_op jit(solution)/shard_map/reduce_scatter | solution.py:278
  729.1 500.0 %reduce-scatter.3.cloned.1.call-start = ((), (), s32[]{:S(2)}) async-start(), calls=%async_computation.3 | async-start | bytes 18579456 | tf_op jit(solution)/shard_map/reduce_scatter | solution.py:277
  814.5 485.4 %all-reduce.185.cloned.1.call-start = ((), (), s32[]{:S(2)}) async-start(), calls=%async_computation.10 | async-start | bytes 6291456 | tf_op jit(solution)/shard_map/psum | solution.py:281
  826.1 45.4 %copy-start.529 = (f32[1952]{0:T(1024)S(1)}, f32[1952]{0:T(1024)}, u32[]{:S(2)}) copy-start(f32[1952]{0:T(1024)} %param.37) | copy-start | bytes 23428
  826.1 47.4 %copy-start.394 = (f32[1952]{0:T(1024)S(1)}, f32[1952]{0:T(1024)}, u32[]{:S(2)}) copy-start(f32[1952]{0:T(1024)} %param.29) | copy-start | bytes 23428
  826.1 48.0 %copy-start.387 = (f32[2,5376]{1,0:T(2,128)S(1)}, f32[2,5376]{1,0:T(2,128)}, u32[]{:S(2)}) copy-start(f32[2,5376]{1,0:T(2,128)} %param.36) | copy-start | bytes 129028
  829.7 399.5 %copy-start.263 = (f32[2,5376]{1,0:T(2,128)S(1)}, f32[2,5376]{1,0:T(2,128)}, u32[]{:S(2)}) copy-start(f32[2,5376]{1,0:T(2,128)} %param.28) | copy-start | bytes 129028
  872.2 430.3 %copy-start.422 = (f32[1952]{0:T(1024)}, f32[1952]{0:T(1024)S(1)}, u32[]{:S(2)}) copy-start(f32[1952]{0:T(1024)S(1)} %get-tuple-element.158) | copy-start | bytes 23428
  874.3 428.2 %copy-start.264 = (f32[2,5376]{1,0:T(2,128)}, f32[2,5376]{1,0:T(2,128)S(1)}, u32[]{:S(2)}) copy-start(f32[2,5376]{1,0:T(2,128)S(1)} %get-tuple-element.160) | copy-start | bytes 129028
  1229.1 75.7 %copy-start.572 = (f32[2,192]{1,0:T(2,128)S(1)}, f32[2,192]{1,0:T(2,128)}, u32[]{:S(2)}) copy-start(f32[2,192]{1,0:T(2,128)} %param.32) | copy-start | bytes 4612
  1229.1 75.9 %copy-start.578 = (f32[48]{0:T(128)S(1)}, f32[48]{0:T(128)}, u32[]{:S(2)}) copy-start(f32[48]{0:T(128)} %param.34) | copy-start | bytes 580
  1229.1 76.5 %copy-start.576 = (f32[2,48]{1,0:T(2,128)S(1)}, f32[2,48]{1,0:T(2,128)}, u32[]{:S(2)}) copy-start(f32[2,48]{1,0:T(2,128)} %param.30) | copy-start | bytes 1156
  1229.1 114.9 %copy-start.342 = (f32[2457]{0:T(1024)S(1)}, f32[2457]{0:T(1024)}, u32[]{:S(2)}) copy-start(f32[2457]{0:T(1024)} %broadcast_multiply_fusion) | copy-start | bytes 29488
  1229.2 114.9 %copy-start.559 = (f32[2,384]{1,0:T(2,128)S(1)}, f32[2,384]{1,0:T(2,128)}, u32[]{:S(2)}) copy-start(f32[2,384]{1,0:T(2,128)} %param.33) | copy-start | bytes 9220
  1229.2 115.0 %copy-start.388 = (f32[2,5376]{1,0:T(2,128)S(1)}, f32[2,5376]{1,0:T(2,128)}, u32[]{:S(2)}) copy-start(f32[2,5376]{1,0:T(2,128)} %param.31) | copy-start | bytes 129028
  1299.8 44.4 %copy-start.131 = (f32[1,48,2457]{2,1,0:T(8,128)S(1)}, f32[1,48,2457]{2,1,0:T(8,128)}, u32[]{:S(2)}) copy-start(f32[1,48,2457]{2,1,0:T(8,128)} %get-tuple-element.156) | copy-start | bytes 1415236
  1299.8 45.2 %copy-start.130 = (f32[2,192,384]{2,1,0:T(8,128)S(1)}, f32[2,192,384]{2,1,0:T(8,128)}, u32[]{:S(2)}) copy-start(f32[2,192,384]{2,1,0:T(8,128)} %get-tuple-element.155) | copy-start | bytes 1769476
  1299.8 45.5 %copy-start.50 = (f32[2,48,5376]{2,1,0:T(8,128)S(1)}, f32[2,48,5376]{2,1,0:T(8,128)}, u32[]{:S(2)}) copy-start(f32[2,48,5376]{2,1,0:T(8,128)} %get-tuple-element.154) | copy-start | bytes 6193156
  1305.0 65.1 %copy-start.479 = (f32[2,192]{1,0:T(2,128)}, f32[2,192]{1,0:T(2,128)S(1)}, u32[]{:S(2)}) copy-start(f32[2,192]{1,0:T(2,128)S(1)} %get-tuple-element.164) | copy-start | bytes 4612
  1305.6 64.4 %copy-start.550 = (f32[48]{0:T(128)}, f32[48]{0:T(128)S(1)}, u32[]{:S(2)}) copy-start(f32[48]{0:T(128)S(1)} %get-tuple-element.162) | copy-start | bytes 580
  1305.7 64.3 %copy-start.526 = (f32[2,48]{1,0:T(2,128)}, f32[2,48]{1,0:T(2,128)S(1)}, u32[]{:S(2)}) copy-start(f32[2,48]{1,0:T(2,128)S(1)} %get-tuple-element.166) | copy-start | bytes 1156
  1344.1 26.0 %copy-start.280 = (f32[2457]{0:T(1024)}, f32[2457]{0:T(1024)S(1)}, u32[]{:S(2)}) copy-start(f32[2457]{0:T(1024)S(1)} %add_reduce_fusion) | copy-start | bytes 29488
  1344.1 26.0 %copy-start.434 = (f32[2,384]{1,0:T(2,128)}, f32[2,384]{1,0:T(2,128)S(1)}, u32[]{:S(2)}) copy-start(f32[2,384]{1,0:T(2,128)S(1)} %multiply_add_fusion.16) | copy-start | bytes 9220
  1344.2 25.9 %copy-start.257 = (f32[2,5376]{1,0:T(2,128)}, f32[2,5376]{1,0:T(2,128)S(1)}, u32[]{:S(2)}) copy-start(f32[2,5376]{1,0:T(2,128)S(1)} %multiply_add_fusion.15) | copy-start | bytes 129028
  (557 other events, 1968.4 us)
Sparse Core Ops, SparseCore 0:
  10.2 43.8 all-gather.17
  56.2 39.7 all-gather.13
  98.3 46.4 all-gather.9
  147.4 70.5 all-gather.11
  220.6 70.4 all-gather.15
  703.0 148.1 all-reduce.182
  854.9 94.8 reduce-scatter.4
  953.7 275.4 reduce-scatter.2
  1232.2 67.5 all-reduce.184
where the time goes:
time: 1390 us; the launch traced here: 1380 us
  waiting for transfers between devices  651 us (47%)
  matrix products  306 us (22%)
  other arithmetic  171 us (12%)
  local copies, waits for them, and re-layouts  128 us (9%)
  blocking collectives  96.2 us (7%)
  between operations  27.5 us (2%)
    dot_general x159, matrix products, mult(): return jnp.einsum(form, left, right, preferred_element_type=jnp.float32)  285 us
    reduce_scatter x1, waiting for transfers between devices, shards(): lax.psum_scatter(grad_in_full, 'fsdp', scatter_dimension=1, tiled=True)  279 us
    all_gather x2, waiting for transfers between devices, fetch_weights(): lax.all_gather(own_in, 'fsdp', axis=0, tiled=True)  119 us
    reduce_scatter x1, waiting for transfers between devices, shards(): lax.psum_scatter(grad_out_full, 'fsdp', scatter_dimension=1, tiled=True)  73.4 us
    psum x1, waiting for transfers between devices, shards(): lax.psum((shard_in, shard_out, shard_edge), 'rep')  69.9 us
    all_gather x2, waiting for transfers between devices, fetch_weights(): lax.all_gather(own_out, 'fsdp', axis=0, tiled=True)  58.8 us
    all_gather x1, waiting for transfers between devices, fetch_weights(): lax.all_gather(edge_mat.astype(jnp.bfloat16), 'fsdp', axis=0, tiled=True)  48.7 us
    psum x1, blocking collectives, shards(): lax.psum((grad_lbias, grad_tbias, loss_sum), ('fsdp', 'rep'))  40.9 us
  transfers between devices with their start and end apart: 9, of which 8 were waited for; matrix products, arithmetic and copies ran while one was open for 13% of the time, Pallas kernels for 0%

commit v1 on v0

--- a/solution.py
+++ b/solution.py
@@ -23,6 +23,13 @@
 clip_level = 1.0
 
 
+def swapped_in(x, mesh_axis, d):
+    devices = lax.axis_size(mesh_axis)
+    blocks = jnp.stack([x for _ in range(devices)])
+    blocks = lax.all_to_all(blocks, mesh_axis, split_axis=0, concat_axis=0)
+    return jnp.concatenate(blocks, axis=d)
+
+
 def round_value(values):
     return lax.optimization_barrier(values.astype(jnp.bfloat16)).astype(jnp.float32)
 
@@ -200,7 +207,7 @@
             )
         else:
             full_in, full_out = (
-                lax.all_gather(own_in, "fsdp", axis=0, tiled=True),
+                swapped_in(own_in, "fsdp", 0),
                 lax.all_gather(own_out, "fsdp", axis=0, tiled=True),
             )
         gathered_in.append(full_in)

time: 1390 us -> 1540 us (1.11)
  matrix products: 306 us -> 423 us
  waiting for transfers between devices: 651 us -> 571 us
  other arithmetic: 171 us -> 232 us
  local copies, waits for them, and re-layouts: 128 us -> 160 us
    dot_general x159 -> x198, matrix products: 285 us -> 375 us  [mult(): return jnp.einsum(form, left, right, preferred_element_type=jnp.float32)]
    reduce_scatter x1, waiting for transfers between devices: 73.4 us -> 0.01 us  [shards(): lax.psum_scatter(grad_out_full, 'fsdp', scatter_dimension=1, tiled=True)]
    reduce_scatter x1, waiting for transfers between devices: 279 us -> 224 us  [shards(): lax.psum_scatter(grad_in_full, 'fsdp', scatter_dimension=1, tiled=True)]
    all_gather x2, waiting for transfers between devices: 58.8 us -> 108 us  [fetch_weights(): lax.all_gather(own_out, 'fsdp', axis=0, tiled=True)]
    convert_element_type x22 -> x40, other arithmetic: 13.7 us -> 46.7 us  [round_value(): values.astype(jnp.bfloat16)]
    sub x6 -> x12, matrix products: 21.3 us -> 47.2 us  [block(): weights_soft = low(jax.nn.softmax(scores, axis=-1))]
    unnamed x1187 -> x1329, local copies, waits for them, and re-layouts: 31.5 us -> 29.2 us
  transfers between devices with their start and end apart: 9 -> 11, of which waited for: 8 -> 7; matrix products, arithmetic and copies ran while one was open for 13% -> 50% of each run, Pallas kernels for 0% -> 0%
where the time goes in v1:
time: 1540 us; the launch traced here: 1530 us
  waiting for transfers between devices  571 us (37%)
  matrix products  423 us (27%)
  other arithmetic  232 us (15%)
  local copies, waits for them, and re-layouts  160 us (10%)
  blocking collectives  99.7 us (6%)
  between operations  28.7 us (2%)
    dot_general x198, matrix products, mult(): return jnp.einsum(form, left, right, preferred_element_type=jnp.float32)  375 us
    reduce_scatter x1, waiting for transfers between devices, shards(): lax.psum_scatter(grad_in_full, 'fsdp', scatter_dimension=1, tiled=True)  224 us
    all_gather x2, waiting for transfers between devices, fetch_weights(): lax.all_gather(own_in, 'fsdp', axis=0, tiled=True)  119 us
    all_gather x2, waiting for transfers between devices, fetch_weights(): lax.all_gather(own_out, 'fsdp', axis=0, tiled=True)  108 us
    psum x1, waiting for transfers between devices, shards(): lax.psum((shard_in, shard_out, shard_edge), 'rep')  69.9 us
    all_gather x1, waiting for transfers between devices, fetch_weights(): lax.all_gather(edge_mat.astype(jnp.bfloat16), 'fsdp', axis=0, tiled=True)  49.2 us
    sub x12, matrix products, block(): weights_soft = low(jax.nn.softmax(scores, axis=-1))  47.2 us
    convert_element_type x40, other arithmetic, round_value(): values.astype(jnp.bfloat16)  46.7 us
  transfers between devices with their start and end apart: 11, of which 7 were waited for; matrix products, arithmetic and copies ran while one was open for 50% of the time, Pallas kernels for 0%

profile of v1, /device:TPU:0, one launch (start us, length us, event | category | flops | bytes accessed | tf_op | source)
XLA Modules:
  0.0 1527.9 jit_solution(3519152667923893285)
XLA Ops:
  13.0 3.4 stack.9
  16.4 7.5 all-to-all-start
  46.4 63.9 %all-gather.12.cloned.1.call-done = bf16[1,1536,384]{2,1,0:T(8,128)(2,1)} async-done(((bf16[1,192,384]{2,1,0:T(8,128)(2,1)}), bf16[1,1536,384]{2,1,0:T(8,128)(2,1)}) %all-gather.12.cloned.1.call-update) | async-done | bytes 1179664 | tf_op jit(solution)/shard_map/all_gather | solution.py:211
  110.3 43.6 %all-gather.14.cloned.1.call-done = bf16[1,1536,384]{2,1,0:T(8,128)(2,1)} async-done(((bf16[1,192,384]{2,1,0:T(8,128)(2,1)}), bf16[1,1536,384]{2,1,0:T(8,128)(2,1)}) %all-gather.14.cloned.1.call-update) | async-done | bytes 1179664 | tf_op jit(solution)/shard_map/all_gather | solution.py:211
  153.9 49.2 %all-gather.10.cloned.1.call-done = bf16[384,2457]{1,0:T(8,128)(2,1)} async-done(((bf16[48,2457]{1,0:T(8,128)(2,1)}), bf16[384,2457]{1,0:T(8,128)(2,1)}) %all-gather.10.cloned.1.call-update) | async-done | bytes 1886992 | tf_op jit(solution)/shard_map/all_gather | solution.py:218
  226.6 49.8 %all-gather.16.cloned.1.call-done = bf16[1,384,5376]{2,1,0:T(8,128)(2,1)} async-done(((bf16[1,48,5376]{2,1,0:T(8,128)(2,1)}), bf16[1,384,5376]{2,1,0:T(8,128)(2,1)}) %all-gather.16.cloned.1.call-update) | async-done | bytes 4128784 | tf_op jit(solution)/shard_map/all_gather | solution.py:205
  280.7 68.9 %all-gather.18.cloned.1.call-done = bf16[1,384,5376]{2,1,0:T(8,128)(2,1)} async-done(((bf16[1,48,5376]{2,1,0:T(8,128)(2,1)}), bf16[1,384,5376]{2,1,0:T(8,128)(2,1)}) %all-gather.18.cloned.1.call-update) | async-done | bytes 4128784 | tf_op jit(solution)/shard_map/all_gather | solution.py:205
  364.1 3.9 fusion.559
  368.1 3.3 divide_convert_fusion.1
  376.7 5.0 multiply_convert_fusion.3
  389.5 4.0 fusion.560
  393.5 3.4 divide_convert_fusion
  402.3 4.6 multiply_convert_fusion.2
  415.8 4.0 fusion.565
  429.0 4.7 multiply_convert_fusion.7
  444.9 4.6 fusion.566
  449.5 3.3 divide_convert_fusion.2
  460.4 4.6 multiply_convert_fusion.6
  477.5 4.7 fusion.562
  482.2 3.4 divide_convert_fusion.5
  493.1 4.6 multiply_convert_fusion.11
  509.1 4.6 fusion.563
  515.0 3.3 divide_convert_fusion.4
  662.1 3.7 multiply_reduce_fusion.45
  727.3 4.7 all-to-all-start.1
  758.6 3.9 multiply_reduce_fusion.23
  776.5 3.9 multiply_reduce_fusion.21
  831.8 6.9 add_bitcast_fusion.6
  838.8 9.1 copy.871
  915.8 5.1 add_bitcast_fusion
  920.9 12.9 add_bitcast_fusion.4
  934.6 11.5 add_bitcast_fusion.1
  946.1 21.0 %add_add_fusion = f32[2,384,5376]{2,1,0:T(8,128)} fusion(f32[1,384,5376]{2,1,0:T(8,128)} %add_bitcast_fusion, f32[1,384,5376]{2,1,0:T(8,128)} %get-tuple-element.548, f32[1,384,5376]{2,1,0:T(8,128)S(1)} %add_bitcast_fusion.2, f32[1,384,5376]{2,1,0:T(8,128)} %get-tuple-element.549, f32[1,384,5376]{2,1,0:T(8,128)} %get-tuple-element.550, ...), kind=kLoop, calls=%fused_computation.21 | loop fusion | flops 20643840 | bytes 66060288 | tf_op jit(solution)/shard_map/add | solution.py:264
  976.3 3.4 fusion.579
  986.4 4.0 fusion.113
  998.4 3.4 fusion.582
  1016.6 3.8 fusion.573
  1020.4 3.4 divide_convert_fusion.9
  1038.8 3.8 fusion.576
  1042.7 3.4 divide_convert_fusion.8
  1061.5 3.4 divide_convert_fusion.7
  1080.2 4.1 fusion.570
  1084.3 3.3 divide_convert_fusion.6
  1104.6 44.3 %all-reduce.176 = (f32[]{:T(128)}, f32[2,5376]{1,0:T(2,128)S(1)}, f32[1952]{0:T(1024)S(1)}) all-reduce(f32[]{:T(128)S(6)} %add.2146, f32[2,5376]{1,0:T(2,128)S(1)} %add_add_fusion.26, f32[1952]{0:T(1024)S(1)} %add_add_fusion.27), channel_id=1, replica_groups=mesh['fsdp'=8,'rep'=4] {'fsdp','rep'}, use_global_device_ids=true, to_apply=%region_50.52 | all-reduce | flops 12705 | bytes 101640 | tf_op jit(solution)/shard_map/psum | solution.py:289
  1153.6 224.1 %reduce-scatter.3.cloned.1.call-done = f32[2,48,5376]{2,1,0:T(8,128)} async-done(((f32[2,384,5376]{2,1,0:T(8,128)}), f32[2,48,5376]{2,1,0:T(8,128)}) %reduce-scatter.3.cloned.1.call-update) | async-done | bytes 2064400 | tf_op jit(solution)/shard_map/reduce_scatter | solution.py:284
  1378.5 69.9 %all-reduce.185.cloned.1.call-done = (f32[2,48,5376]{2,1,0:T(8,128)}, f32[2,192,384]{2,1,0:T(8,128)}, f32[1,48,2457]{2,1,0:T(8,128)}) async-done(((f32[2,48,5376]{2,1,0:T(8,128)}, f32[2,192,384]{2,1,0:T(8,128)}, f32[1,48,2457]{2,1,0:T(8,128)}), (f32[2,48,5376]{2,1,0:T(8,128)}, f32[2,192,384]{2,1,0:T(8,128)}, f32[1,48,2457]{2,1,0:T(8,128)})) %all-reduce.185.cloned.1.call-update) | async-done | bytes 3125968 | tf_op jit(solution)/shard_map/psum | solution.py:288
  1454.3 37.6 %all-reduce.178 = (f32[2]{0:T(128)S(1)}, f32[2,5376]{1,0:T(2,128)S(1)}, f32[2]{0:T(128)S(1)}, f32[2,384]{1,0:T(2,128)S(1)}, f32[1]{0:T(128)}, /*index=5*/f32[1,2457]{1,0:T(1,128)S(1)}) all-reduce(f32[2]{0:T(128)S(1)} %get-tuple-element.165, f32[2,5376]{1,0:T(2,128)S(1)} %get-tuple-element.73, ...), channel_id=1, replica_groups=mesh['fsdp'=8,'rep'=4] {'fsdp'}, use_global_device_ids=true, to_apply=%region_159.162 | all-reduce | flops 13982 | bytes 111856 | tf_op jit(solution)/shard_map/psum | solution.py:308
  1494.5 17.8 %all-reduce.177 = (f32[2]{0:T(128)S(1)}, f32[2]{0:T(128)S(1)}, f32[1]{0:T(128)}) all-reduce(f32[2]{0:T(128)S(1)} %multiply_reduce_fusion.18, f32[2]{0:T(128)S(1)} %multiply_reduce_fusion.88, f32[1]{0:T(128)} %bitcast.216), channel_id=1, replica_groups=mesh['fsdp'=8,'rep'=4] {'fsdp'}, use_global_device_ids=true, to_apply=%region_161.164 | all-reduce | flops 5 | bytes 40 | tf_op jit(solution)/shard_map/psum | solution.py:325
  (2019 shorter events, 634.3 us)
Async XLA Ops:
  7.2 103.1 %all-gather.12.cloned.1.call-start = ((), (), s32[]{:S(2)}) async-start(), calls=%async_computation.7 | async-start | bytes 1327104 | tf_op jit(solution)/shard_map/all_gather | solution.py:211
  9.2 144.7 %all-gather.14.cloned.1.call-start = ((), (), s32[]{:S(2)}) async-start(), calls=%async_computation.8 | async-start | bytes 1327104 | tf_op jit(solution)/shard_map/all_gather | solution.py:211
  10.0 193.2 %all-gather.10.cloned.1.call-start = ((), (), s32[]{:S(2)}) async-start(), calls=%async_computation.4 | async-start | bytes 2211840 | tf_op jit(solution)/shard_map/all_gather | solution.py:218
  11.8 264.6 %all-gather.16.cloned.1.call-start = ((), (), s32[]{:S(2)}) async-start(), calls=%async_computation.9 | async-start | bytes 4644864 | tf_op jit(solution)/shard_map/all_gather | solution.py:205
  16.4 708.7 %all-to-all-start = ((bf16[8,48,5376]{2,1,0:T(8,128)(2,1)}), bf16[8,48,5376]{2,1,0:T(8,128)(2,1)}, u32[]{:S(2)}, u32[]{:S(2)}) async-start(bf16[8,48,5376]{2,1,0:T(8,128)(2,1)} %stack.9), calls=%async_computation | async-start | bytes 8257536 | tf_op jit(solution)/shard_map/all_to_all | solution.py:29
  23.8 325.8 %all-gather.18.cloned.1.call-start = ((), (), s32[]{:S(2)}) async-start(), calls=%async_computation.10 | async-start | bytes 4644864 | tf_op jit(solution)/shard_map/all_gather | solution.py:205
  29.0 175.3 %copy-start.619 = (bf16[2,256]{1,0:T(2,128)(2,1)}, bf16[2,256]{1,0:T(2,128)(2,1)S(1)}, u32[]{:S(2)}) copy-start(bf16[2,256]{1,0:T(2,128)(2,1)S(1)} %pad_maximum_fusion.5) | copy-start | bytes 3076
  31.9 177.3 %copy-start.621 = (bf16[2,256]{1,0:T(2,128)(2,1)}, bf16[2,256]{1,0:T(2,128)(2,1)S(1)}, u32[]{:S(2)}) copy-start(bf16[2,256]{1,0:T(2,128)(2,1)S(1)} %pad_maximum_fusion.4) | copy-start | bytes 3076
  34.2 179.3 %copy-start.623 = (bf16[2,256]{1,0:T(2,128)(2,1)}, bf16[2,256]{1,0:T(2,128)(2,1)S(1)}, u32[]{:S(2)}) copy-start(bf16[2,256]{1,0:T(2,128)(2,1)S(1)} %pad_maximum_fusion.3) | copy-start | bytes 3076
  42.7 356.4 %copy-start.294 = (f32[384]{0:T(512)}, f32[384]{0:T(512)S(1)}, u32[]{:S(2)}) copy-start(f32[384]{0:T(512)S(1)} %get-tuple-element.125) | copy-start | bytes 4612
  43.9 310.5 %copy-start.230 = (f32[2304]{0:T(1024)}, f32[2304]{0:T(1024)S(1)}, u32[]{:S(2)}) copy-start(f32[2304]{0:T(1024)S(1)} %get-tuple-element.135) | copy-start | bytes 27652
  44.0 312.9 %copy-start.228 = (f32[2304]{0:T(1024)}, f32[2304]{0:T(1024)S(1)}, u32[]{:S(2)}) copy-start(f32[2304]{0:T(1024)S(1)} %get-tuple-element.134) | copy-start | bytes 27652
  45.8 160.4 %copy-start.641 = (f32[384]{0:T(512)}, f32[384]{0:T(512)S(1)}, u32[]{:S(2)}) copy-start(f32[384]{0:T(512)S(1)} %get-tuple-element.358) | copy-start | bytes 4612
  209.2 140.3 %copy-start.312 = (bf16[2,384]{1,0:T(2,128)(2,1)}, bf16[2,384]{1,0:T(2,128)(2,1)S(1)}, u32[]{:S(2)}) copy-start(bf16[2,384]{1,0:T(2,128)(2,1)S(1)} %get-tuple-element.223) | copy-start | bytes 4612
  213.5 138.5 %copy-start.315 = (bf16[2,384]{1,0:T(2,128)(2,1)}, bf16[2,384]{1,0:T(2,128)(2,1)S(1)}, u32[]{:S(2)}) copy-start(bf16[2,384]{1,0:T(2,128)(2,1)S(1)} %get-tuple-element.219) | copy-start | bytes 4612
  217.9 139.0 %copy-start.319 = (bf16[2,384]{1,0:T(2,128)(2,1)}, bf16[2,384]{1,0:T(2,128)(2,1)S(1)}, u32[]{:S(2)}) copy-start(bf16[2,384]{1,0:T(2,128)(2,1)S(1)} %get-tuple-element.215) | copy-start | bytes 4612
  219.3 154.3 %copy-start = (f32[2,256,384]{2,1,0:T(8,128)}, f32[2,256,384]{2,1,0:T(8,128)S(1)}, u32[]{:S(2)}) copy-start(f32[2,256,384]{2,1,0:T(8,128)S(1)} %get-tuple-element.411) | copy-start | bytes 2359300
  219.4 140.6 %copy-start.375 = (f32[2,256]{1,0:T(2,128)}, f32[2,256]{1,0:T(2,128)S(1)}, u32[]{:S(2)}) copy-start(f32[2,256]{1,0:T(2,128)S(1)} %broadcast_multiply_fusion.17) | copy-start | bytes 6148
  219.6 58.6 %copy-start.492 = (f32[2,256]{1,0:T(2,128)}, f32[2,256]{1,0:T(2,128)S(1)}, u32[]{:S(2)}) copy-start(f32[2,256]{1,0:T(2,128)S(1)} %multiply_reduce_fusion.77) | copy-start | bytes 6148
  221.0 204.3 %copy-start.3 = (f32[2,256,384]{2,1,0:T(8,128)}, f32[2,256,384]{2,1,0:T(8,128)S(1)}, u32[]{:S(2)}) copy-start(f32[2,256,384]{2,1,0:T(8,128)S(1)} %get-tuple-element.444) | copy-start | bytes 2359300
  221.9 58.8 %copy-start.494 = (f32[2,256]{1,0:T(2,128)}, f32[2,256]{1,0:T(2,128)S(1)}, u32[]{:S(2)}) copy-start(f32[2,256]{1,0:T(2,128)S(1)} %multiply_reduce_fusion.82) | copy-start | bytes 6148
  222.4 54.0 %copy-start.382 = (f32[2,256]{1,0:T(2,128)}, f32[2,256]{1,0:T(2,128)S(1)}, u32[]{:S(2)}) copy-start(f32[2,256]{1,0:T(2,128)S(1)} %broadcast_multiply_fusion.27) | copy-start | bytes 6148
  222.6 129.4 %copy-start.496 = (f32[2,256]{1,0:T(2,128)}, f32[2,256]{1,0:T(2,128)S(1)}, u32[]{:S(2)}) copy-start(f32[2,256]{1,0:T(2,128)S(1)} %multiply_reduce_fusion.87) | copy-start | bytes 6148
  222.7 137.3 %copy-start.467 = (f32[2,256]{1,0:T(2,128)}, f32[2,256]{1,0:T(2,128)S(1)}, u32[]{:S(2)}) copy-start(f32[2,256]{1,0:T(2,128)S(1)} %fusion.437) | copy-start | bytes 6148
  727.3 263.1 %all-to-all-start.1 = ((bf16[8,48,5376]{2,1,0:T(8,128)(2,1)}), bf16[8,48,5376]{2,1,0:T(8,128)(2,1)}, u32[]{:S(2)}, u32[]{:S(2)}) async-start(bf16[8,48,5376]{2,1,0:T(8,128)(2,1)} %stack.11), calls=%async_computation.1 | async-start | bytes 8257536 | tf_op jit(solution)/shard_map/all_to_all | solution.py:29
  732.1 419.7 %all-reduce.183.cloned.1.call-start = ((), (), s32[]{:S(2)}) async-start(), calls=%async_computation.11 | async-start | bytes 7864320
  847.9 305.7 %reduce-scatter.5.cloned.1.call-start = ((), (), s32[]{:S(2)}) async-start(), calls=%async_computation.6 | async-start | bytes 5308416 | tf_op jit(solution)/shard_map/reduce_scatter | solution.py:285
  876.9 500.8 %reduce-scatter.3.cloned.1.call-start = ((), (), s32[]{:S(2)}) async-start(), calls=%async_computation.5 | async-start | bytes 18579456 | tf_op jit(solution)/shard_map/reduce_scatter | solution.py:284
  967.2 481.2 %all-reduce.185.cloned.1.call-start = ((), (), s32[]{:S(2)}) async-start(), calls=%async_computation.12 | async-start | bytes 6291456 | tf_op jit(solution)/shard_map/psum | solution.py:288
  1096.0 52.9 %copy-start.578 = (f32[1952]{0:T(1024)S(1)}, f32[1952]{0:T(1024)}, u32[]{:S(2)}) copy-start(f32[1952]{0:T(1024)} %param.37) | copy-start | bytes 23428
  1096.0 54.9 %copy-start.447 = (f32[1952]{0:T(1024)S(1)}, f32[1952]{0:T(1024)}, u32[]{:S(2)}) copy-start(f32[1952]{0:T(1024)} %param.29) | copy-start | bytes 23428
  1096.0 55.5 %copy-start.440 = (f32[2,5376]{1,0:T(2,128)S(1)}, f32[2,5376]{1,0:T(2,128)}, u32[]{:S(2)}) copy-start(f32[2,5376]{1,0:T(2,128)} %param.36) | copy-start | bytes 129028
  1103.5 274.2 %copy-start.267 = (f32[2,5376]{1,0:T(2,128)S(1)}, f32[2,5376]{1,0:T(2,128)}, u32[]{:S(2)}) copy-start(f32[2,5376]{1,0:T(2,128)} %param.28) | copy-start | bytes 129028
  1149.6 301.3 %copy-start.466 = (f32[1952]{0:T(1024)}, f32[1952]{0:T(1024)S(1)}, u32[]{:S(2)}) copy-start(f32[1952]{0:T(1024)S(1)} %get-tuple-element.158) | copy-start | bytes 23428
  1151.7 299.2 %copy-start.268 = (f32[2,5376]{1,0:T(2,128)}, f32[2,5376]{1,0:T(2,128)S(1)}, u32[]{:S(2)}) copy-start(f32[2,5376]{1,0:T(2,128)S(1)} %get-tuple-element.160) | copy-start | bytes 129028
  1377.7 75.7 %copy-start.649 = (f32[2,48]{1,0:T(2,128)S(1)}, f32[2,48]{1,0:T(2,128)}, u32[]{:S(2)}) copy-start(f32[2,48]{1,0:T(2,128)} %param.30) | copy-start | bytes 1156
  1377.7 75.8 %copy-start.650 = (f32[48]{0:T(128)S(1)}, f32[48]{0:T(128)}, u32[]{:S(2)}) copy-start(f32[48]{0:T(128)} %param.34) | copy-start | bytes 580
  1377.7 76.4 %copy-start.639 = (f32[2,192]{1,0:T(2,128)S(1)}, f32[2,192]{1,0:T(2,128)}, u32[]{:S(2)}) copy-start(f32[2,192]{1,0:T(2,128)} %param.32) | copy-start | bytes 4612
  1377.7 114.2 %copy-start.392 = (f32[2457]{0:T(1024)S(1)}, f32[2457]{0:T(1024)}, u32[]{:S(2)}) copy-start(f32[2457]{0:T(1024)} %broadcast_multiply_fusion) | copy-start | bytes 29488
  1377.7 114.9 %copy-start.630 = (f32[2,384]{1,0:T(2,128)S(1)}, f32[2,384]{1,0:T(2,128)}, u32[]{:S(2)}) copy-start(f32[2,384]{1,0:T(2,128)} %param.33) | copy-start | bytes 9220
  1377.7 114.9 %copy-start.441 = (f32[2,5376]{1,0:T(2,128)S(1)}, f32[2,5376]{1,0:T(2,128)}, u32[]{:S(2)}) copy-start(f32[2,5376]{1,0:T(2,128)} %param.31) | copy-start | bytes 129028
  1448.4 44.4 %copy-start.119 = (f32[1,48,2457]{2,1,0:T(8,128)S(1)}, f32[1,48,2457]{2,1,0:T(8,128)}, u32[]{:S(2)}) copy-start(f32[1,48,2457]{2,1,0:T(8,128)} %get-tuple-element.156) | copy-start | bytes 1415236
  1448.4 45.2 %copy-start.115 = (f32[2,192,384]{2,1,0:T(8,128)S(1)}, f32[2,192,384]{2,1,0:T(8,128)}, u32[]{:S(2)}) copy-start(f32[2,192,384]{2,1,0:T(8,128)} %get-tuple-element.155) | copy-start | bytes 1769476
  1448.4 45.5 %copy-start.27 = (f32[2,48,5376]{2,1,0:T(8,128)S(1)}, f32[2,48,5376]{2,1,0:T(8,128)}, u32[]{:S(2)}) copy-start(f32[2,48,5376]{2,1,0:T(8,128)} %get-tuple-element.154) | copy-start | bytes 6193156
  1453.5 63.8 %copy-start.575 = (f32[2,48]{1,0:T(2,128)}, f32[2,48]{1,0:T(2,128)S(1)}, u32[]{:S(2)}) copy-start(f32[2,48]{1,0:T(2,128)S(1)} %get-tuple-element.166) | copy-start | bytes 1156
  1454.1 63.1 %copy-start.616 = (f32[48]{0:T(128)}, f32[48]{0:T(128)S(1)}, u32[]{:S(2)}) copy-start(f32[48]{0:T(128)S(1)} %get-tuple-element.162) | copy-start | bytes 580
  1454.3 63.0 %copy-start.521 = (f32[2,192]{1,0:T(2,128)}, f32[2,192]{1,0:T(2,128)S(1)}, u32[]{:S(2)}) copy-start(f32[2,192]{1,0:T(2,128)S(1)} %get-tuple-element.164) | copy-start | bytes 4612
  1491.9 25.3 %copy-start.293 = (f32[2457]{0:T(1024)}, f32[2457]{0:T(1024)S(1)}, u32[]{:S(2)}) copy-start(f32[2457]{0:T(1024)S(1)} %add_reduce_fusion) | copy-start | bytes 29488
  (629 other events, 2794.7 us)
Sparse Core Ops, SparseCore 0:
  10.2 100.0 all-gather.11
  112.5 41.4 all-gather.13
  156.7 46.4 all-gather.9
  205.8 70.5 all-gather.15
  279.0 70.4 all-gather.17
  848.0 150.7 all-reduce.182
  1002.5 94.6 reduce-scatter.4
  1101.2 276.4 reduce-scatter.2
  1380.8 67.5 all-reduce.184
